TPU v7x, 32 devices: a whole 2x2x4 slice. The times are simulated.
32 devices in a mesh: sec: 4 (over y, x), bond: 8 (over z, core).
Axes of the slice: x: 2, y: 2, z: 4, core: 2. Of those that a mesh axis runs over, the one named last changes fastest.
Arguments:
- left_vectors: bfloat16 [128, 4096], P(None, 'bond'), may hold values from -6 to 6
- site_tensors: bfloat16 [4, 4096, 4, 4096], P('sec', None, None, 'bond'), may hold values from -0.09375 to 0.09375
- displacement: float32 [128, 216], P('sec'), may hold values from -2.5 to 2.5
- photon_counts: int32 [128, 216], P('sec'), may hold values from 0 to 3
- mode_order: int32 [216], replicated, may hold values from 0 to 215, each once
Outputs:
- log_likelihood: float32 [4, 128], P('sec')
- log_norm: float32 [4, 128], P('sec')
Inputs may be any that keep to these rules, and one draw needn't show every extreme that they name: `mode_order`: each of the 216 modes appears once.
All inputs are finite; a program needn't handle non-finite values.
Results may differ from a plain program's by a relative error of at most 0.0015.
Values may be sent and summed in bfloat16 or wider, within the bound.
No kernel may reach another device: no remote copies, remote signals or barrier semaphores. Data moves between devices by JAX's collectives and lax.ppermute only.
A program may use at most 64 MiB of HBM per device.

v0:
```python
import math
import jax
import jax.numpy as jnp
from jax import lax
from jax.sharding import PartitionSpec as P

CUT = 4
epsilon = 1e-06


def passed_along(x, axis, by):
    size = lax.axis_size(axis)
    pairs = [(i, i + by) for i in range(size) if 0 <= i + by < size]
    return lax.ppermute(x, axis, pairs)


def displacement_table(cutoff):
    table = [
        [[0.0 for degree_slot in range(2 * cutoff - 1)] for col_level in range(cutoff)]
        for row_level in range(cutoff)
    ]
    for row_level in range(cutoff):
        for col_level in range(cutoff):
            lower = min(row_level, col_level)
            upper = max(row_level, col_level)
            excess = upper - lower
            parity = 1.0 if row_level >= col_level else (-1.0) ** excess
            prefactor = math.sqrt(math.factorial(lower) / math.factorial(upper))
            for term in range(lower + 1):
                table[row_level][col_level][excess + 2 * term] += (
                    parity
                    * prefactor
                    * (-1.0) ** term
                    * math.comb(upper, lower - term)
                    / math.factorial(term)
                )
    return table


def displacement_matrix(amplitude):
    table = jnp.asarray(displacement_table(CUT), dtype=jnp.float32)
    power_list = [jnp.ones_like(amplitude)]
    for degree in range(2 * CUT - 2):
        power_list.append(power_list[-1] * amplitude)
    power_stack = jnp.stack(power_list, axis=1)
    poly = jnp.einsum("sp,mnp->smn", power_stack, table, precision=lax.Precision.HIGHEST)
    return jnp.exp(-0.5 * amplitude * amplitude)[:, None, None] * poly


def local(left_vectors, site_tensors, displacement, photon_counts, mode_order):
    full_width = site_tensors.shape[1]
    cutoff = site_tensors.shape[2]
    local_width = site_tensors.shape[3]
    samples = left_vectors.shape[0]
    segment_count = lax.axis_size("sec")
    segment_index = lax.axis_index("sec")
    matrix = site_tensors.reshape(full_width, cutoff * local_width)
    stacked = jnp.stack([displacement, photon_counts.astype(jnp.float32)])
    mode_total = displacement.shape[1]
    window_order = mode_order[:segment_count]
    picker = (window_order[None, :] == jnp.arange(mode_total, dtype=jnp.int32)[:, None]).astype(
        jnp.float32
    )
    ordered = jnp.einsum("rsm,mj->rsj", stacked, picker, precision=lax.Precision.HIGHEST)
    columns = lax.all_to_all(ordered, "sec", split_axis=2, concat_axis=1, tiled=True)
    matrices_all = displacement_matrix(columns[0, :, 0])
    counts_all = columns[1, :, 0]
    levels = jnp.arange(cutoff).astype(jnp.float32)
    blocks = 4
    block_rows = samples // blocks
    incoming_zero = jnp.zeros((block_rows, local_width), jnp.float32)
    extra_zero = jnp.zeros((block_rows,), jnp.float32)

    def add_rows(fragment):
        return jnp.dot(fragment, matrix, preferred_element_type=jnp.float32)

    def one_step(turn_index, state):
        incoming, extra_in, record, norm_record = state
        block_index = turn_index - segment_index
        usable = (block_index >= 0) & (block_index < blocks)
        clamped = jnp.clip(block_index, 0, blocks - 1)
        first_row = clamped * block_rows
        opening = lax.dynamic_slice_in_dim(left_vectors, first_row, block_rows, 0)
        source = jnp.where(segment_index == 0, opening, incoming.astype(jnp.bfloat16))
        factor = jnp.where(segment_index == 0, jnp.ones_like(extra_in), extra_in)
        projected = add_rows(lax.all_gather(source, "bond", axis=1, tiled=True))
        projected = (projected * factor[:, None]).reshape(block_rows, cutoff, local_width)
        shifts = lax.dynamic_slice_in_dim(matrices_all, first_row, block_rows, 0)
        counted = lax.dynamic_slice_in_dim(counts_all, first_row, block_rows, 0)
        displaced = jnp.einsum("smn,snb->smb", shifts, projected, precision=lax.Precision.HIGHEST)
        partial_value = jnp.sum(displaced * displaced, axis=2)
        weights = lax.psum(partial_value, "bond")
        select = (counted[:, None] == levels[None, :]).astype(jnp.float32)
        chosen_weight = jnp.sum(select * weights, axis=1)
        log_prob = jnp.log(chosen_weight) - jnp.log(jnp.sum(weights, axis=1))
        log_scale = jnp.log(chosen_weight / full_width + epsilon)
        chosen = jnp.sum(select[:, :, None] * displaced, axis=1)
        next_vector = chosen.astype(jnp.bfloat16)
        previous = lax.dynamic_slice_in_dim(record, first_row, block_rows, 0)
        record = lax.dynamic_update_slice_in_dim(
            record, jnp.where(usable, log_prob, previous), first_row, 0
        )
        previous_norm = lax.dynamic_slice_in_dim(norm_record, first_row, block_rows, 0)
        norm_record = lax.dynamic_update_slice_in_dim(
            norm_record, jnp.where(usable, log_scale, previous_norm), first_row, 0
        )
        extra_out = lax.rsqrt(chosen_weight / full_width + epsilon)
        incoming, extra_next = passed_along((next_vector.astype(jnp.float32), extra_out), "sec", 1)
        return (incoming, extra_next, record, norm_record)

    record_zero = jnp.zeros((samples,), jnp.float32)
    final_state = lax.fori_loop(
        0,
        segment_count + blocks - 1,
        one_step,
        (incoming_zero, extra_zero, record_zero, record_zero),
    )
    return (final_state[2][None, :], final_state[3][None, :])


def solution(mesh):
    placed = (P(None, "bond"), P("sec", None, None, "bond"), P("sec", None), P("sec", None), P())
    return jax.shard_map(
        local,
        mesh=mesh,
        in_specs=placed,
        out_specs=(P("sec", None), P("sec", None)),
        check_vma=False,
    )
```

profile of v0, /device:TPU:0, one launch (start us, length us, event | category | flops | bytes accessed | tf_op | source)
XLA Modules:
  0.0 450.2 jit_solution(1115947929308692932)
XLA Ops:
  0.6 0.8 convert_bitcast_fusion
  1.4 0.7 slice.11
  2.1 0.9 fusion.6
  3.0 0.7 copy.9
  3.7 5.2 %all-to-all-start = ((f32[2,32,4]{1,0,2:T(2,128)}), f32[2,32,4]{1,0,2:T(2,128)S(1)}, u32[]{:S(2)}, u32[]{:S(2)}) async-start(f32[2,32,4]{1,0,2:T(2,128)} %copy.9), calls=%async_computation | async-start | bytes 8192 | tf_op jit(solution)/shard_map/all_to_all | solution.py:65
  8.8 16.9 %copy.12 = bf16[512,8,4,512]{3,1,2,0:T(8,128)(2,1)} copy(bf16[512,8,4,512]{3,2,1,0:T(4,128)(2,1)} %bitcast.32) | data formatting | bytes 33554432
  26.3 423.5 %while.21 = (s32[]{:T(128)}, bf16[32,512]{1,0:T(8,128)(2,1)S(1)}, f32[32]{0:T(128)S(1)}, f32[128]{0:T(128)S(1)}, f32[128]{0:T(128)S(1)}, /*index=5*/s32[]{:T(128...) while((s32[]{:T(128)}, bf16[32,512]{1,0:T(8,128)(2,1)S(1)}, ...), condition=%wide.region_6.7_spmd.clone, body=%wide.region_0.6_spmd.clone.sunk | while | flops 540345216 | bytes 18662804 | solution.py:112
  26.3 0.8 convert_select_fusion.2
  27.1 14.4 %all_gather.10 = bf16[32,4096]{1,0:T(8,128)(2,1)S(1)} all-gather(bf16[32,512]{1,0:T(8,128)(2,1)S(1)} %convert_select_fusion.2), channel_id=1, replica_groups=mesh['sec'=4,'bond'=8] {'bond'}, dimensions={1}, use_global_device_ids=true | all-gather | bytes 294912 | tf_op jit(solution)/shard_map/while/body/eval_jaxpr/all_gather | solution.py:86
  41.5 8.8 %convolution_multiply_fusion.3 = f32[32,2048]{1,0:T(8,128)S(1)} fusion(bf16[32,4096]{1,0:T(8,128)(2,1)S(1)} %all_gather.10, bf16[4096,2048]{1,0:T(8,128)(2,1)} %get-tuple-element.446, f32[32]{0:T(128)S(1)} %broadcast_select_fusion.4), kind=kOutput, calls=%fused_computation.1.clone.1 | convolution fusion | flops 536936448 | bytes 17301632 | tf_op jit(solution)/shard_map/while/body/eval_jaxpr/dot_general | solution.py:75
  50.8 0.8 multiply_reduce_fusion.3
  51.6 3.9 collective-permute-start
  55.6 28.8 %psum.14 = f32[32,4]{1,0:T(8,128)S(1)} all-reduce(f32[32,4]{1,0:T(8,128)S(1)} %get-tuple-element.396), channel_id=1, replica_groups=mesh['sec'=4,'bond'=8] {'bond'}, use_global_device_ids=true, to_apply=%region_3.3 | all-reduce | flops 128 | bytes 1024 | tf_op jit(solution)/shard_map/while/body/eval_jaxpr/psum | solution.py:92
  84.8 3.4 collective-permute-start.1
  88.1 1.3 collective-permute-done.1
  89.4 0.8 convert_select_fusion.2
  90.2 14.2 %all_gather.10 = bf16[32,4096]{1,0:T(8,128)(2,1)S(1)} all-gather(bf16[32,512]{1,0:T(8,128)(2,1)S(1)} %convert_select_fusion.2), channel_id=1, replica_groups=mesh['sec'=4,'bond'=8] {'bond'}, dimensions={1}, use_global_device_ids=true | all-gather | bytes 294912 | tf_op jit(solution)/shard_map/while/body/eval_jaxpr/all_gather | solution.py:86
  104.4 8.8 %convolution_multiply_fusion.3 = f32[32,2048]{1,0:T(8,128)S(1)} fusion(bf16[32,4096]{1,0:T(8,128)(2,1)S(1)} %all_gather.10, bf16[4096,2048]{1,0:T(8,128)(2,1)} %get-tuple-element.446, f32[32]{0:T(128)S(1)} %broadcast_select_fusion.4), kind=kOutput, calls=%fused_computation.1.clone.1 | convolution fusion | flops 536936448 | bytes 17301632 | tf_op jit(solution)/shard_map/while/body/eval_jaxpr/dot_general | solution.py:75
  113.7 0.8 multiply_reduce_fusion.3
  114.5 4.2 collective-permute-start
  118.7 25.9 %psum.14 = f32[32,4]{1,0:T(8,128)S(1)} all-reduce(f32[32,4]{1,0:T(8,128)S(1)} %get-tuple-element.396), channel_id=1, replica_groups=mesh['sec'=4,'bond'=8] {'bond'}, use_global_device_ids=true, to_apply=%region_3.3 | all-reduce | flops 128 | bytes 1024 | tf_op jit(solution)/shard_map/while/body/eval_jaxpr/psum | solution.py:92
  145.0 4.3 collective-permute-start.1
  149.2 1.3 collective-permute-done.1
  150.5 0.8 convert_select_fusion.2
  151.3 14.2 %all_gather.10 = bf16[32,4096]{1,0:T(8,128)(2,1)S(1)} all-gather(bf16[32,512]{1,0:T(8,128)(2,1)S(1)} %convert_select_fusion.2), channel_id=1, replica_groups=mesh['sec'=4,'bond'=8] {'bond'}, dimensions={1}, use_global_device_ids=true | all-gather | bytes 294912 | tf_op jit(solution)/shard_map/while/body/eval_jaxpr/all_gather | solution.py:86
  165.5 8.8 %convolution_multiply_fusion.3 = f32[32,2048]{1,0:T(8,128)S(1)} fusion(bf16[32,4096]{1,0:T(8,128)(2,1)S(1)} %all_gather.10, bf16[4096,2048]{1,0:T(8,128)(2,1)} %get-tuple-element.446, f32[32]{0:T(128)S(1)} %broadcast_select_fusion.4), kind=kOutput, calls=%fused_computation.1.clone.1 | convolution fusion | flops 536936448 | bytes 17301632 | tf_op jit(solution)/shard_map/while/body/eval_jaxpr/dot_general | solution.py:75
  174.8 0.8 multiply_reduce_fusion.3
  175.6 4.2 collective-permute-start
  179.8 25.9 %psum.14 = f32[32,4]{1,0:T(8,128)S(1)} all-reduce(f32[32,4]{1,0:T(8,128)S(1)} %get-tuple-element.396), channel_id=1, replica_groups=mesh['sec'=4,'bond'=8] {'bond'}, use_global_device_ids=true, to_apply=%region_3.3 | all-reduce | flops 128 | bytes 1024 | tf_op jit(solution)/shard_map/while/body/eval_jaxpr/psum | solution.py:92
  206.0 3.0 collective-permute-start.1
  209.1 1.3 collective-permute-done.1
  210.3 0.8 convert_select_fusion.2
  211.1 14.2 %all_gather.10 = bf16[32,4096]{1,0:T(8,128)(2,1)S(1)} all-gather(bf16[32,512]{1,0:T(8,128)(2,1)S(1)} %convert_select_fusion.2), channel_id=1, replica_groups=mesh['sec'=4,'bond'=8] {'bond'}, dimensions={1}, use_global_device_ids=true | all-gather | bytes 294912 | tf_op jit(solution)/shard_map/while/body/eval_jaxpr/all_gather | solution.py:86
  225.3 8.8 %convolution_multiply_fusion.3 = f32[32,2048]{1,0:T(8,128)S(1)} fusion(bf16[32,4096]{1,0:T(8,128)(2,1)S(1)} %all_gather.10, bf16[4096,2048]{1,0:T(8,128)(2,1)} %get-tuple-element.446, f32[32]{0:T(128)S(1)} %broadcast_select_fusion.4), kind=kOutput, calls=%fused_computation.1.clone.1 | convolution fusion | flops 536936448 | bytes 17301632 | tf_op jit(solution)/shard_map/while/body/eval_jaxpr/dot_general | solution.py:75
  234.6 0.8 multiply_reduce_fusion.3
  235.4 4.2 collective-permute-start
  239.6 25.9 %psum.14 = f32[32,4]{1,0:T(8,128)S(1)} all-reduce(f32[32,4]{1,0:T(8,128)S(1)} %get-tuple-element.396), channel_id=1, replica_groups=mesh['sec'=4,'bond'=8] {'bond'}, use_global_device_ids=true, to_apply=%region_3.3 | all-reduce | flops 128 | bytes 1024 | tf_op jit(solution)/shard_map/while/body/eval_jaxpr/psum | solution.py:92
  265.9 3.0 collective-permute-start.1
  268.9 1.3 collective-permute-done.1
  270.2 0.8 convert_select_fusion.2
  271.0 14.2 %all_gather.10 = bf16[32,4096]{1,0:T(8,128)(2,1)S(1)} all-gather(bf16[32,512]{1,0:T(8,128)(2,1)S(1)} %convert_select_fusion.2), channel_id=1, replica_groups=mesh['sec'=4,'bond'=8] {'bond'}, dimensions={1}, use_global_device_ids=true | all-gather | bytes 294912 | tf_op jit(solution)/shard_map/while/body/eval_jaxpr/all_gather | solution.py:86
  285.2 8.8 %convolution_multiply_fusion.3 = f32[32,2048]{1,0:T(8,128)S(1)} fusion(bf16[32,4096]{1,0:T(8,128)(2,1)S(1)} %all_gather.10, bf16[4096,2048]{1,0:T(8,128)(2,1)} %get-tuple-element.446, f32[32]{0:T(128)S(1)} %broadcast_select_fusion.4), kind=kOutput, calls=%fused_computation.1.clone.1 | convolution fusion | flops 536936448 | bytes 17301632 | tf_op jit(solution)/shard_map/while/body/eval_jaxpr/dot_general | solution.py:75
  294.4 0.8 multiply_reduce_fusion.3
  295.3 4.2 collective-permute-start
  299.4 25.9 %psum.14 = f32[32,4]{1,0:T(8,128)S(1)} all-reduce(f32[32,4]{1,0:T(8,128)S(1)} %get-tuple-element.396), channel_id=1, replica_groups=mesh['sec'=4,'bond'=8] {'bond'}, use_global_device_ids=true, to_apply=%region_3.3 | all-reduce | flops 128 | bytes 1024 | tf_op jit(solution)/shard_map/while/body/eval_jaxpr/psum | solution.py:92
  325.7 3.0 collective-permute-start.1
  328.8 1.3 collective-permute-done.1
  330.0 0.8 convert_select_fusion.2
  330.8 14.2 %all_gather.10 = bf16[32,4096]{1,0:T(8,128)(2,1)S(1)} all-gather(bf16[32,512]{1,0:T(8,128)(2,1)S(1)} %convert_select_fusion.2), channel_id=1, replica_groups=mesh['sec'=4,'bond'=8] {'bond'}, dimensions={1}, use_global_device_ids=true | all-gather | bytes 294912 | tf_op jit(solution)/shard_map/while/body/eval_jaxpr/all_gather | solution.py:86
  345.0 8.8 %convolution_multiply_fusion.3 = f32[32,2048]{1,0:T(8,128)S(1)} fusion(bf16[32,4096]{1,0:T(8,128)(2,1)S(1)} %all_gather.10, bf16[4096,2048]{1,0:T(8,128)(2,1)} %get-tuple-element.446, f32[32]{0:T(128)S(1)} %broadcast_select_fusion.4), kind=kOutput, calls=%fused_computation.1.clone.1 | convolution fusion | flops 536936448 | bytes 17301632 | tf_op jit(solution)/shard_map/while/body/eval_jaxpr/dot_general | solution.py:75
  354.3 0.8 multiply_reduce_fusion.3
  355.1 4.2 collective-permute-start
  359.3 25.9 %psum.14 = f32[32,4]{1,0:T(8,128)S(1)} all-reduce(f32[32,4]{1,0:T(8,128)S(1)} %get-tuple-element.396), channel_id=1, replica_groups=mesh['sec'=4,'bond'=8] {'bond'}, use_global_device_ids=true, to_apply=%region_3.3 | all-reduce | flops 128 | bytes 1024 | tf_op jit(solution)/shard_map/while/body/eval_jaxpr/psum | solution.py:92
  385.6 3.0 collective-permute-start.1
  388.6 1.3 collective-permute-done.1
  389.9 0.8 convert_select_fusion.2
  390.6 14.2 %all_gather.10 = bf16[32,4096]{1,0:T(8,128)(2,1)S(1)} all-gather(bf16[32,512]{1,0:T(8,128)(2,1)S(1)} %convert_select_fusion.2), channel_id=1, replica_groups=mesh['sec'=4,'bond'=8] {'bond'}, dimensions={1}, use_global_device_ids=true | all-gather | bytes 294912 | tf_op jit(solution)/shard_map/while/body/eval_jaxpr/all_gather | solution.py:86
  404.8 8.8 %convolution_multiply_fusion.3 = f32[32,2048]{1,0:T(8,128)S(1)} fusion(bf16[32,4096]{1,0:T(8,128)(2,1)S(1)} %all_gather.10, bf16[4096,2048]{1,0:T(8,128)(2,1)} %get-tuple-element.446, f32[32]{0:T(128)S(1)} %broadcast_select_fusion.4), kind=kOutput, calls=%fused_computation.1.clone.1 | convolution fusion | flops 536936448 | bytes 17301632 | tf_op jit(solution)/shard_map/while/body/eval_jaxpr/dot_general | solution.py:75
  414.1 0.8 multiply_reduce_fusion.3
  414.9 4.2 collective-permute-start
  419.1 25.9 %psum.14 = f32[32,4]{1,0:T(8,128)S(1)} all-reduce(f32[32,4]{1,0:T(8,128)S(1)} %get-tuple-element.396), channel_id=1, replica_groups=mesh['sec'=4,'bond'=8] {'bond'}, use_global_device_ids=true, to_apply=%region_3.3 | all-reduce | flops 128 | bytes 1024 | tf_op jit(solution)/shard_map/while/body/eval_jaxpr/psum | solution.py:92
  445.4 3.0 collective-permute-start.1
  448.4 1.3 collective-permute-done.1
  449.7 0.5 copy-done
  (89 shorter events, 6.6 us)
Async XLA Ops:
  3.7 22.1 %all-to-all-start = ((f32[2,32,4]{1,0,2:T(2,128)}), f32[2,32,4]{1,0,2:T(2,128)S(1)}, u32[]{:S(2)}, u32[]{:S(2)}) async-start(f32[2,32,4]{1,0,2:T(2,128)} %copy.9), calls=%async_computation | async-start | bytes 8192 | tf_op jit(solution)/shard_map/all_to_all | solution.py:65
  8.8 17.2 %copy-start.2 = (f32[4,4,7]{2,1,0:T(4,128)S(1)}, f32[4,4,7]{2,1,0:T(4,128)}, u32[]{:S(2)}) copy-start(f32[4,4,7]{2,1,0:T(4,128)} %constant.99.clone) | copy-start | bytes 1348
  51.6 37.8 %collective-permute-start = (bf16[32,512]{1,0:T(8,128)(2,1)S(1)}, bf16[32,512]{1,0:T(8,128)(2,1)S(1)}, u32[]{:S(2)}, u32[]{:S(2)}) collective-permute-start(bf16[32,512]{1,0:T(8,128)(2,1)S(1)} %get-tuple-element.395), channel_id=1, source_target_pairs={{0,8},{8,16},{16,24},{1,9},{9,17},{17,25},{2,10},{10,18},{18,26},{... | collective-permute-start | bytes 98312 | tf_op jit(solution)/shard_map/while/body/eval_jaxpr/ppermute | solution.py:14
  84.8 4.7 %collective-permute-start.1 = (f32[32]{0:T(128)S(1)}, f32[32]{0:T(128)S(1)}, u32[]{:S(2)}, u32[]{:S(2)}) collective-permute-start(f32[32]{0:T(128)S(1)} %get-tuple-element.399), channel_id=1, source_target_pairs={{0,8},{8,16},{16,24},{1,9},{9,17},{17,25},{2,10},{10,18},{18,26},{... | collective-permute-start | bytes 392 | tf_op jit(solution)/shard_map/while/body/eval_jaxpr/ppermute | solution.py:14
  114.5 36.0 %collective-permute-start = (bf16[32,512]{1,0:T(8,128)(2,1)S(1)}, bf16[32,512]{1,0:T(8,128)(2,1)S(1)}, u32[]{:S(2)}, u32[]{:S(2)}) collective-permute-start(bf16[32,512]{1,0:T(8,128)(2,1)S(1)} %get-tuple-element.395), channel_id=1, source_target_pairs={{0,8},{8,16},{16,24},{1,9},{9,17},{17,25},{2,10},{10,18},{18,26},{... | collective-permute-start | bytes 98312 | tf_op jit(solution)/shard_map/while/body/eval_jaxpr/ppermute | solution.py:14
  145.0 5.5 %collective-permute-start.1 = (f32[32]{0:T(128)S(1)}, f32[32]{0:T(128)S(1)}, u32[]{:S(2)}, u32[]{:S(2)}) collective-permute-start(f32[32]{0:T(128)S(1)} %get-tuple-element.399), channel_id=1, source_target_pairs={{0,8},{8,16},{16,24},{1,9},{9,17},{17,25},{2,10},{10,18},{18,26},{... | collective-permute-start | bytes 392 | tf_op jit(solution)/shard_map/while/body/eval_jaxpr/ppermute | solution.py:14
  175.6 34.8 %collective-permute-start = (bf16[32,512]{1,0:T(8,128)(2,1)S(1)}, bf16[32,512]{1,0:T(8,128)(2,1)S(1)}, u32[]{:S(2)}, u32[]{:S(2)}) collective-permute-start(bf16[32,512]{1,0:T(8,128)(2,1)S(1)} %get-tuple-element.395), channel_id=1, source_target_pairs={{0,8},{8,16},{16,24},{1,9},{9,17},{17,25},{2,10},{10,18},{18,26},{... | collective-permute-start | bytes 98312 | tf_op jit(solution)/shard_map/while/body/eval_jaxpr/ppermute | solution.py:14
  206.0 4.3 collective-permute-start.1
  235.4 34.8 %collective-permute-start = (bf16[32,512]{1,0:T(8,128)(2,1)S(1)}, bf16[32,512]{1,0:T(8,128)(2,1)S(1)}, u32[]{:S(2)}, u32[]{:S(2)}) collective-permute-start(bf16[32,512]{1,0:T(8,128)(2,1)S(1)} %get-tuple-element.395), channel_id=1, source_target_pairs={{0,8},{8,16},{16,24},{1,9},{9,17},{17,25},{2,10},{10,18},{18,26},{... | collective-permute-start | bytes 98312 | tf_op jit(solution)/shard_map/while/body/eval_jaxpr/ppermute | solution.py:14
  265.9 4.3 collective-permute-start.1
  295.3 34.8 %collective-permute-start = (bf16[32,512]{1,0:T(8,128)(2,1)S(1)}, bf16[32,512]{1,0:T(8,128)(2,1)S(1)}, u32[]{:S(2)}, u32[]{:S(2)}) collective-permute-start(bf16[32,512]{1,0:T(8,128)(2,1)S(1)} %get-tuple-element.395), channel_id=1, source_target_pairs={{0,8},{8,16},{16,24},{1,9},{9,17},{17,25},{2,10},{10,18},{18,26},{... | collective-permute-start | bytes 98312 | tf_op jit(solution)/shard_map/while/body/eval_jaxpr/ppermute | solution.py:14
  325.7 4.3 collective-permute-start.1
  355.1 34.8 %collective-permute-start = (bf16[32,512]{1,0:T(8,128)(2,1)S(1)}, bf16[32,512]{1,0:T(8,128)(2,1)S(1)}, u32[]{:S(2)}, u32[]{:S(2)}) collective-permute-start(bf16[32,512]{1,0:T(8,128)(2,1)S(1)} %get-tuple-element.395), channel_id=1, source_target_pairs={{0,8},{8,16},{16,24},{1,9},{9,17},{17,25},{2,10},{10,18},{18,26},{... | collective-permute-start | bytes 98312 | tf_op jit(solution)/shard_map/while/body/eval_jaxpr/ppermute | solution.py:14
  385.6 4.3 collective-permute-start.1
  414.9 34.8 %collective-permute-start = (bf16[32,512]{1,0:T(8,128)(2,1)S(1)}, bf16[32,512]{1,0:T(8,128)(2,1)S(1)}, u32[]{:S(2)}, u32[]{:S(2)}) collective-permute-start(bf16[32,512]{1,0:T(8,128)(2,1)S(1)} %get-tuple-element.395), channel_id=1, source_target_pairs={{0,8},{8,16},{16,24},{1,9},{9,17},{17,25},{2,10},{10,18},{18,26},{... | collective-permute-start | bytes 98312 | tf_op jit(solution)/shard_map/while/body/eval_jaxpr/ppermute | solution.py:14
  445.4 4.3 collective-permute-start.1
  449.7 0.5 copy-start
  449.7 0.5 copy-start.1
where the time goes:
time: 452 us; the launch traced here: 450 us
  blocking collectives  284 us (63%)
  matrix products  68 us (15%)
  starting transfers between devices  56.8 us (13%)
  local copies, waits for them, and re-layouts  22.2 us (5%)
  other arithmetic  9.19 us (2%)
  waiting for transfers between devices  8.94 us (2%)
    psum x7, blocking collectives, one_step(): weights = lax.psum(partial_value, 'bond')  184 us
    all_gather x7, blocking collectives, one_step(): projected = add_rows(lax.all_gather(source, 'bond', axis=1, tiled=True))  99.6 us
    dot_general x7, matrix products, add_rows(): return jnp.dot(fragment, matrix, preferred_element_type=jnp.float32)  61.3 us
    ppermute x14, starting transfers between devices, passed_along(): return lax.ppermute(x, axis, pairs)  51.6 us
    unnamed x7, local copies, waits for them, and re-layouts  17.4 us
  transfers between devices with their start and end apart: 15, of which 7 were waited for; matrix products, arithmetic and copies ran while one was open for 4% of the time, Pallas kernels for 0%

commit v1 on v0

--- a/solution.py
+++ b/solution.py
@@ -89,7 +89,7 @@
         counted = lax.dynamic_slice_in_dim(counts_all, first_row, block_rows, 0)
         displaced = jnp.einsum("smn,snb->smb", shifts, projected, precision=lax.Precision.HIGHEST)
         partial_value = jnp.sum(displaced * displaced, axis=2)
-        weights = lax.psum(partial_value, "bond")
+        weights = jnp.sum(lax.all_gather(partial_value, "bond"), axis=0)
         select = (counted[:, None] == levels[None, :]).astype(jnp.float32)
         chosen_weight = jnp.sum(select * weights, axis=1)
         log_prob = jnp.log(chosen_weight) - jnp.log(jnp.sum(weights, axis=1))

time: 452 us -> 356 us (0.79)
  blocking collectives: 284 us -> 189 us
    psum x7 -> x0, blocking collectives: 184 us -> none  [one_step(): weights = lax.psum(partial_value, 'bond')]
    all_gather x0 -> x7, blocking collectives: none -> 89.4 us  [one_step(): weights = jnp.sum(lax.all_gather(partial_value, 'bond'), axis=0)]
  transfers between devices with their start and end apart: 15 -> 15, of which waited for: 7 -> 7; matrix products, arithmetic and copies ran while one was open for 4% -> 5% of each run, Pallas kernels for 0% -> 0%
where the time goes in v1:
time: 356 us; the launch traced here: 355 us
  blocking collectives  189 us (53%)
  matrix products  68.1 us (19%)
  starting transfers between devices  55.8 us (16%)
  local copies, waits for them, and re-layouts  23.4 us (7%)
  waiting for transfers between devices  8.94 us (3%)
  other arithmetic  8.62 us (2%)
    all_gather x7, blocking collectives, one_step(): projected = add_rows(lax.all_gather(source, 'bond', axis=1, tiled=True))  99.6 us
    all_gather x7, blocking collectives, one_step(): weights = jnp.sum(lax.all_gather(partial_value, 'bond'), axis=0)  89.4 us
    dot_general x7, matrix products, add_rows(): return jnp.dot(fragment, matrix, preferred_element_type=jnp.float32)  61.3 us
    ppermute x14, starting transfers between devices, passed_along(): return lax.ppermute(x, axis, pairs)  50.6 us
    unnamed x7, local copies, waits for them, and re-layouts  17.4 us
    ppermute x14, waiting for transfers between devices, passed_along(): return lax.ppermute(x, axis, pairs)  8.93 us
  transfers between devices with their start and end apart: 15, of which 7 were waited for; matrix products, arithmetic and copies ran while one was open for 5% of the time, Pallas kernels for 0%

profile of v1, /device:TPU:0, one launch (start us, length us, event | category | flops | bytes accessed | tf_op | source)
XLA Modules:
  0.0 354.8 jit_solution(5637536636743607543)
XLA Ops:
  0.6 0.8 convert_bitcast_fusion
  1.4 0.7 slice.11
  2.1 0.9 fusion.6
  3.0 0.7 copy.11
  3.7 5.2 %all-to-all-start = ((f32[2,32,4]{1,0,2:T(2,128)}), f32[2,32,4]{1,0,2:T(2,128)S(1)}, u32[]{:S(2)}, u32[]{:S(2)}) async-start(f32[2,32,4]{1,0,2:T(2,128)} %copy.11), calls=%async_computation | async-start | bytes 8192 | tf_op jit(solution)/shard_map/all_to_all | solution.py:65
  8.8 16.9 %copy.14 = bf16[512,8,4,512]{3,1,2,0:T(8,128)(2,1)} copy(bf16[512,8,4,512]{3,2,1,0:T(4,128)(2,1)} %bitcast.35) | data formatting | bytes 33554432
  26.3 328.0 %while.21 = (s32[]{:T(128)}, bf16[32,512]{1,0:T(8,128)(2,1)S(1)}, f32[32]{0:T(128)S(1)}, f32[128]{0:T(128)S(1)}, f32[128]{0:T(128)S(1)}, /*index=5*/s32[]{:T(128...) while((s32[]{:T(128)}, bf16[32,512]{1,0:T(8,128)(2,1)S(1)}, ...), condition=%wide.region_6.7_spmd.clone, body=%wide.region_0.6_spmd.clone.sunk | while | flops 540346880 | bytes 18673044 | solution.py:112
  26.3 0.8 convert_select_fusion.2
  27.1 14.4 %all_gather.26 = bf16[32,4096]{1,0:T(8,128)(2,1)S(1)} all-gather(bf16[32,512]{1,0:T(8,128)(2,1)S(1)} %convert_select_fusion.2), channel_id=1, replica_groups=mesh['sec'=4,'bond'=8] {'bond'}, dimensions={1}, use_global_device_ids=true | all-gather | bytes 294912 | tf_op jit(solution)/shard_map/while/body/eval_jaxpr/all_gather | solution.py:86
  41.5 8.8 %convolution_multiply_fusion.3 = f32[32,2048]{1,0:T(8,128)S(1)} fusion(bf16[32,4096]{1,0:T(8,128)(2,1)S(1)} %all_gather.26, bf16[4096,2048]{1,0:T(8,128)(2,1)} %get-tuple-element.446, f32[32]{0:T(128)S(1)} %broadcast_select_fusion.4), kind=kOutput, calls=%fused_computation.1.clone.1 | convolution fusion | flops 536936448 | bytes 17301632 | tf_op jit(solution)/shard_map/while/body/eval_jaxpr/dot_general | solution.py:75
  50.9 0.8 multiply_reduce_fusion.3
  51.7 3.9 %collective-permute-start = (bf16[32,512]{1,0:T(8,128)(2,1)S(1)}, bf16[32,512]{1,0:T(8,128)(2,1)S(1)}, u32[]{:S(2)}, u32[]{:S(2)}) collective-permute-start(bf16[32,512]{1,0:T(8,128)(2,1)S(1)} %get-tuple-element.395), channel_id=1, source_target_pairs={{0,8},{8,16},{16,24},{1,9},{9,17},{17,25},{2,10},{10,18},{18,26},{... | collective-permute-start | bytes 98312 | tf_op jit(solution)/shard_map/while/body/eval_jaxpr/ppermute | solution.py:14
  55.7 12.8 %all-gather.4 = f32[8,32,4]{1,2,0:T(4,128)S(1)} all-gather(f32[1,32,4]{1,2,0:T(4,128)S(1)} %bitcast.36), channel_id=2, replica_groups=mesh['sec'=4,'bond'=8] {'bond'}, dimensions={0}, use_global_device_ids=true | all-gather | bytes 4608 | tf_op jit(solution)/shard_map/while/body/eval_jaxpr/all_gather | solution.py:92
  68.8 3.4 collective-permute-start.1
  72.1 1.3 collective-permute-done.1
  73.4 0.8 convert_select_fusion.2
  74.2 14.2 %all_gather.26 = bf16[32,4096]{1,0:T(8,128)(2,1)S(1)} all-gather(bf16[32,512]{1,0:T(8,128)(2,1)S(1)} %convert_select_fusion.2), channel_id=1, replica_groups=mesh['sec'=4,'bond'=8] {'bond'}, dimensions={1}, use_global_device_ids=true | all-gather | bytes 294912 | tf_op jit(solution)/shard_map/while/body/eval_jaxpr/all_gather | solution.py:86
  88.4 8.8 %convolution_multiply_fusion.3 = f32[32,2048]{1,0:T(8,128)S(1)} fusion(bf16[32,4096]{1,0:T(8,128)(2,1)S(1)} %all_gather.26, bf16[4096,2048]{1,0:T(8,128)(2,1)} %get-tuple-element.446, f32[32]{0:T(128)S(1)} %broadcast_select_fusion.4), kind=kOutput, calls=%fused_computation.1.clone.1 | convolution fusion | flops 536936448 | bytes 17301632 | tf_op jit(solution)/shard_map/while/body/eval_jaxpr/dot_general | solution.py:75
  97.8 0.8 multiply_reduce_fusion.3
  98.6 4.2 %collective-permute-start = (bf16[32,512]{1,0:T(8,128)(2,1)S(1)}, bf16[32,512]{1,0:T(8,128)(2,1)S(1)}, u32[]{:S(2)}, u32[]{:S(2)}) collective-permute-start(bf16[32,512]{1,0:T(8,128)(2,1)S(1)} %get-tuple-element.395), channel_id=1, source_target_pairs={{0,8},{8,16},{16,24},{1,9},{9,17},{17,25},{2,10},{10,18},{18,26},{... | collective-permute-start | bytes 98312 | tf_op jit(solution)/shard_map/while/body/eval_jaxpr/ppermute | solution.py:14
  102.8 12.8 %all-gather.4 = f32[8,32,4]{1,2,0:T(4,128)S(1)} all-gather(f32[1,32,4]{1,2,0:T(4,128)S(1)} %bitcast.36), channel_id=2, replica_groups=mesh['sec'=4,'bond'=8] {'bond'}, dimensions={0}, use_global_device_ids=true | all-gather | bytes 4608 | tf_op jit(solution)/shard_map/while/body/eval_jaxpr/all_gather | solution.py:92
  115.9 4.3 %collective-permute-start.1 = (f32[32]{0:T(128)S(1)}, f32[32]{0:T(128)S(1)}, u32[]{:S(2)}, u32[]{:S(2)}) collective-permute-start(f32[32]{0:T(128)S(1)} %get-tuple-element.399), channel_id=1, source_target_pairs={{0,8},{8,16},{16,24},{1,9},{9,17},{17,25},{2,10},{10,18},{18,26},{... | collective-permute-start | bytes 392 | tf_op jit(solution)/shard_map/while/body/eval_jaxpr/ppermute | solution.py:14
  120.1 1.3 collective-permute-done.1
  121.4 0.8 convert_select_fusion.2
  122.2 14.2 %all_gather.26 = bf16[32,4096]{1,0:T(8,128)(2,1)S(1)} all-gather(bf16[32,512]{1,0:T(8,128)(2,1)S(1)} %convert_select_fusion.2), channel_id=1, replica_groups=mesh['sec'=4,'bond'=8] {'bond'}, dimensions={1}, use_global_device_ids=true | all-gather | bytes 294912 | tf_op jit(solution)/shard_map/while/body/eval_jaxpr/all_gather | solution.py:86
  136.4 8.8 %convolution_multiply_fusion.3 = f32[32,2048]{1,0:T(8,128)S(1)} fusion(bf16[32,4096]{1,0:T(8,128)(2,1)S(1)} %all_gather.26, bf16[4096,2048]{1,0:T(8,128)(2,1)} %get-tuple-element.446, f32[32]{0:T(128)S(1)} %broadcast_select_fusion.4), kind=kOutput, calls=%fused_computation.1.clone.1 | convolution fusion | flops 536936448 | bytes 17301632 | tf_op jit(solution)/shard_map/while/body/eval_jaxpr/dot_general | solution.py:75
  145.8 0.8 multiply_reduce_fusion.3
  146.6 4.2 %collective-permute-start = (bf16[32,512]{1,0:T(8,128)(2,1)S(1)}, bf16[32,512]{1,0:T(8,128)(2,1)S(1)}, u32[]{:S(2)}, u32[]{:S(2)}) collective-permute-start(bf16[32,512]{1,0:T(8,128)(2,1)S(1)} %get-tuple-element.395), channel_id=1, source_target_pairs={{0,8},{8,16},{16,24},{1,9},{9,17},{17,25},{2,10},{10,18},{18,26},{... | collective-permute-start | bytes 98312 | tf_op jit(solution)/shard_map/while/body/eval_jaxpr/ppermute | solution.py:14
  150.8 12.8 %all-gather.4 = f32[8,32,4]{1,2,0:T(4,128)S(1)} all-gather(f32[1,32,4]{1,2,0:T(4,128)S(1)} %bitcast.36), channel_id=2, replica_groups=mesh['sec'=4,'bond'=8] {'bond'}, dimensions={0}, use_global_device_ids=true | all-gather | bytes 4608 | tf_op jit(solution)/shard_map/while/body/eval_jaxpr/all_gather | solution.py:92
  163.9 2.8 collective-permute-start.1
  166.7 1.3 collective-permute-done.1
  168.0 0.8 convert_select_fusion.2
  168.8 14.2 %all_gather.26 = bf16[32,4096]{1,0:T(8,128)(2,1)S(1)} all-gather(bf16[32,512]{1,0:T(8,128)(2,1)S(1)} %convert_select_fusion.2), channel_id=1, replica_groups=mesh['sec'=4,'bond'=8] {'bond'}, dimensions={1}, use_global_device_ids=true | all-gather | bytes 294912 | tf_op jit(solution)/shard_map/while/body/eval_jaxpr/all_gather | solution.py:86
  183.0 8.8 %convolution_multiply_fusion.3 = f32[32,2048]{1,0:T(8,128)S(1)} fusion(bf16[32,4096]{1,0:T(8,128)(2,1)S(1)} %all_gather.26, bf16[4096,2048]{1,0:T(8,128)(2,1)} %get-tuple-element.446, f32[32]{0:T(128)S(1)} %broadcast_select_fusion.4), kind=kOutput, calls=%fused_computation.1.clone.1 | convolution fusion | flops 536936448 | bytes 17301632 | tf_op jit(solution)/shard_map/while/body/eval_jaxpr/dot_general | solution.py:75
  192.3 0.8 multiply_reduce_fusion.3
  193.2 4.2 %collective-permute-start = (bf16[32,512]{1,0:T(8,128)(2,1)S(1)}, bf16[32,512]{1,0:T(8,128)(2,1)S(1)}, u32[]{:S(2)}, u32[]{:S(2)}) collective-permute-start(bf16[32,512]{1,0:T(8,128)(2,1)S(1)} %get-tuple-element.395), channel_id=1, source_target_pairs={{0,8},{8,16},{16,24},{1,9},{9,17},{17,25},{2,10},{10,18},{18,26},{... | collective-permute-start | bytes 98312 | tf_op jit(solution)/shard_map/while/body/eval_jaxpr/ppermute | solution.py:14
  197.4 12.8 %all-gather.4 = f32[8,32,4]{1,2,0:T(4,128)S(1)} all-gather(f32[1,32,4]{1,2,0:T(4,128)S(1)} %bitcast.36), channel_id=2, replica_groups=mesh['sec'=4,'bond'=8] {'bond'}, dimensions={0}, use_global_device_ids=true | all-gather | bytes 4608 | tf_op jit(solution)/shard_map/while/body/eval_jaxpr/all_gather | solution.py:92
  210.5 2.8 collective-permute-start.1
  213.3 1.3 collective-permute-done.1
  214.6 0.8 convert_select_fusion.2
  215.3 14.2 %all_gather.26 = bf16[32,4096]{1,0:T(8,128)(2,1)S(1)} all-gather(bf16[32,512]{1,0:T(8,128)(2,1)S(1)} %convert_select_fusion.2), channel_id=1, replica_groups=mesh['sec'=4,'bond'=8] {'bond'}, dimensions={1}, use_global_device_ids=true | all-gather | bytes 294912 | tf_op jit(solution)/shard_map/while/body/eval_jaxpr/all_gather | solution.py:86
  229.5 8.8 %convolution_multiply_fusion.3 = f32[32,2048]{1,0:T(8,128)S(1)} fusion(bf16[32,4096]{1,0:T(8,128)(2,1)S(1)} %all_gather.26, bf16[4096,2048]{1,0:T(8,128)(2,1)} %get-tuple-element.446, f32[32]{0:T(128)S(1)} %broadcast_select_fusion.4), kind=kOutput, calls=%fused_computation.1.clone.1 | convolution fusion | flops 536936448 | bytes 17301632 | tf_op jit(solution)/shard_map/while/body/eval_jaxpr/dot_general | solution.py:75
  238.9 0.8 multiply_reduce_fusion.3
  239.7 4.2 %collective-permute-start = (bf16[32,512]{1,0:T(8,128)(2,1)S(1)}, bf16[32,512]{1,0:T(8,128)(2,1)S(1)}, u32[]{:S(2)}, u32[]{:S(2)}) collective-permute-start(bf16[32,512]{1,0:T(8,128)(2,1)S(1)} %get-tuple-element.395), channel_id=1, source_target_pairs={{0,8},{8,16},{16,24},{1,9},{9,17},{17,25},{2,10},{10,18},{18,26},{... | collective-permute-start | bytes 98312 | tf_op jit(solution)/shard_map/while/body/eval_jaxpr/ppermute | solution.py:14
  244.0 12.8 %all-gather.4 = f32[8,32,4]{1,2,0:T(4,128)S(1)} all-gather(f32[1,32,4]{1,2,0:T(4,128)S(1)} %bitcast.36), channel_id=2, replica_groups=mesh['sec'=4,'bond'=8] {'bond'}, dimensions={0}, use_global_device_ids=true | all-gather | bytes 4608 | tf_op jit(solution)/shard_map/while/body/eval_jaxpr/all_gather | solution.py:92
  257.0 2.8 collective-permute-start.1
  259.8 1.3 collective-permute-done.1
  261.1 0.8 convert_select_fusion.2
  261.9 14.2 %all_gather.26 = bf16[32,4096]{1,0:T(8,128)(2,1)S(1)} all-gather(bf16[32,512]{1,0:T(8,128)(2,1)S(1)} %convert_select_fusion.2), channel_id=1, replica_groups=mesh['sec'=4,'bond'=8] {'bond'}, dimensions={1}, use_global_device_ids=true | all-gather | bytes 294912 | tf_op jit(solution)/shard_map/while/body/eval_jaxpr/all_gather | solution.py:86
  276.1 8.8 %convolution_multiply_fusion.3 = f32[32,2048]{1,0:T(8,128)S(1)} fusion(bf16[32,4096]{1,0:T(8,128)(2,1)S(1)} %all_gather.26, bf16[4096,2048]{1,0:T(8,128)(2,1)} %get-tuple-element.446, f32[32]{0:T(128)S(1)} %broadcast_select_fusion.4), kind=kOutput, calls=%fused_computation.1.clone.1 | convolution fusion | flops 536936448 | bytes 17301632 | tf_op jit(solution)/shard_map/while/body/eval_jaxpr/dot_general | solution.py:75
  285.5 0.8 multiply_reduce_fusion.3
  286.3 4.2 %collective-permute-start = (bf16[32,512]{1,0:T(8,128)(2,1)S(1)}, bf16[32,512]{1,0:T(8,128)(2,1)S(1)}, u32[]{:S(2)}, u32[]{:S(2)}) collective-permute-start(bf16[32,512]{1,0:T(8,128)(2,1)S(1)} %get-tuple-element.395), channel_id=1, source_target_pairs={{0,8},{8,16},{16,24},{1,9},{9,17},{17,25},{2,10},{10,18},{18,26},{... | collective-permute-start | bytes 98312 | tf_op jit(solution)/shard_map/while/body/eval_jaxpr/ppermute | solution.py:14
  290.6 12.8 %all-gather.4 = f32[8,32,4]{1,2,0:T(4,128)S(1)} all-gather(f32[1,32,4]{1,2,0:T(4,128)S(1)} %bitcast.36), channel_id=2, replica_groups=mesh['sec'=4,'bond'=8] {'bond'}, dimensions={0}, use_global_device_ids=true | all-gather | bytes 4608 | tf_op jit(solution)/shard_map/while/body/eval_jaxpr/all_gather | solution.py:92
  303.6 2.8 collective-permute-start.1
  306.4 1.3 collective-permute-done.1
  307.7 0.8 convert_select_fusion.2
  308.5 14.2 %all_gather.26 = bf16[32,4096]{1,0:T(8,128)(2,1)S(1)} all-gather(bf16[32,512]{1,0:T(8,128)(2,1)S(1)} %convert_select_fusion.2), channel_id=1, replica_groups=mesh['sec'=4,'bond'=8] {'bond'}, dimensions={1}, use_global_device_ids=true | all-gather | bytes 294912 | tf_op jit(solution)/shard_map/while/body/eval_jaxpr/all_gather | solution.py:86
  322.7 8.8 %convolution_multiply_fusion.3 = f32[32,2048]{1,0:T(8,128)S(1)} fusion(bf16[32,4096]{1,0:T(8,128)(2,1)S(1)} %all_gather.26, bf16[4096,2048]{1,0:T(8,128)(2,1)} %get-tuple-element.446, f32[32]{0:T(128)S(1)} %broadcast_select_fusion.4), kind=kOutput, calls=%fused_computation.1.clone.1 | convolution fusion | flops 536936448 | bytes 17301632 | tf_op jit(solution)/shard_map/while/body/eval_jaxpr/dot_general | solution.py:75
  332.0 0.8 multiply_reduce_fusion.3
  332.9 4.2 %collective-permute-start = (bf16[32,512]{1,0:T(8,128)(2,1)S(1)}, bf16[32,512]{1,0:T(8,128)(2,1)S(1)}, u32[]{:S(2)}, u32[]{:S(2)}) collective-permute-start(bf16[32,512]{1,0:T(8,128)(2,1)S(1)} %get-tuple-element.395), channel_id=1, source_target_pairs={{0,8},{8,16},{16,24},{1,9},{9,17},{17,25},{2,10},{10,18},{18,26},{... | collective-permute-start | bytes 98312 | tf_op jit(solution)/shard_map/while/body/eval_jaxpr/ppermute | solution.py:14
  337.1 12.8 %all-gather.4 = f32[8,32,4]{1,2,0:T(4,128)S(1)} all-gather(f32[1,32,4]{1,2,0:T(4,128)S(1)} %bitcast.36), channel_id=2, replica_groups=mesh['sec'=4,'bond'=8] {'bond'}, dimensions={0}, use_global_device_ids=true | all-gather | bytes 4608 | tf_op jit(solution)/shard_map/while/body/eval_jaxpr/all_gather | solution.py:92
  350.2 2.8 collective-permute-start.1
  353.0 1.3 collective-permute-done.1
  354.3 0.5 copy-done
  (110 shorter events, 7.2 us)
Async XLA Ops:
  3.7 22.1 %all-to-all-start = ((f32[2,32,4]{1,0,2:T(2,128)}), f32[2,32,4]{1,0,2:T(2,128)S(1)}, u32[]{:S(2)}, u32[]{:S(2)}) async-start(f32[2,32,4]{1,0,2:T(2,128)} %copy.11), calls=%async_computation | async-start | bytes 8192 | tf_op jit(solution)/shard_map/all_to_all | solution.py:65
  8.8 17.2 %copy-start.2 = (f32[4,4,7]{2,1,0:T(4,128)S(1)}, f32[4,4,7]{2,1,0:T(4,128)}, u32[]{:S(2)}) copy-start(f32[4,4,7]{2,1,0:T(4,128)} %constant.99.clone) | copy-start | bytes 1348
  51.7 21.7 %collective-permute-start = (bf16[32,512]{1,0:T(8,128)(2,1)S(1)}, bf16[32,512]{1,0:T(8,128)(2,1)S(1)}, u32[]{:S(2)}, u32[]{:S(2)}) collective-permute-start(bf16[32,512]{1,0:T(8,128)(2,1)S(1)} %get-tuple-element.395), channel_id=1, source_target_pairs={{0,8},{8,16},{16,24},{1,9},{9,17},{17,25},{2,10},{10,18},{18,26},{... | collective-permute-start | bytes 98312 | tf_op jit(solution)/shard_map/while/body/eval_jaxpr/ppermute | solution.py:14
  68.8 4.7 %collective-permute-start.1 = (f32[32]{0:T(128)S(1)}, f32[32]{0:T(128)S(1)}, u32[]{:S(2)}, u32[]{:S(2)}) collective-permute-start(f32[32]{0:T(128)S(1)} %get-tuple-element.399), channel_id=1, source_target_pairs={{0,8},{8,16},{16,24},{1,9},{9,17},{17,25},{2,10},{10,18},{18,26},{... | collective-permute-start | bytes 392 | tf_op jit(solution)/shard_map/while/body/eval_jaxpr/ppermute | solution.py:14
  98.6 22.8 %collective-permute-start = (bf16[32,512]{1,0:T(8,128)(2,1)S(1)}, bf16[32,512]{1,0:T(8,128)(2,1)S(1)}, u32[]{:S(2)}, u32[]{:S(2)}) collective-permute-start(bf16[32,512]{1,0:T(8,128)(2,1)S(1)} %get-tuple-element.395), channel_id=1, source_target_pairs={{0,8},{8,16},{16,24},{1,9},{9,17},{17,25},{2,10},{10,18},{18,26},{... | collective-permute-start | bytes 98312 | tf_op jit(solution)/shard_map/while/body/eval_jaxpr/ppermute | solution.py:14
  115.9 5.5 %collective-permute-start.1 = (f32[32]{0:T(128)S(1)}, f32[32]{0:T(128)S(1)}, u32[]{:S(2)}, u32[]{:S(2)}) collective-permute-start(f32[32]{0:T(128)S(1)} %get-tuple-element.399), channel_id=1, source_target_pairs={{0,8},{8,16},{16,24},{1,9},{9,17},{17,25},{2,10},{10,18},{18,26},{... | collective-permute-start | bytes 392 | tf_op jit(solution)/shard_map/while/body/eval_jaxpr/ppermute | solution.py:14
  146.6 21.4 %collective-permute-start = (bf16[32,512]{1,0:T(8,128)(2,1)S(1)}, bf16[32,512]{1,0:T(8,128)(2,1)S(1)}, u32[]{:S(2)}, u32[]{:S(2)}) collective-permute-start(bf16[32,512]{1,0:T(8,128)(2,1)S(1)} %get-tuple-element.395), channel_id=1, source_target_pairs={{0,8},{8,16},{16,24},{1,9},{9,17},{17,25},{2,10},{10,18},{18,26},{... | collective-permute-start | bytes 98312 | tf_op jit(solution)/shard_map/while/body/eval_jaxpr/ppermute | solution.py:14
  163.9 4.1 %collective-permute-start.1 = (f32[32]{0:T(128)S(1)}, f32[32]{0:T(128)S(1)}, u32[]{:S(2)}, u32[]{:S(2)}) collective-permute-start(f32[32]{0:T(128)S(1)} %get-tuple-element.399), channel_id=1, source_target_pairs={{0,8},{8,16},{16,24},{1,9},{9,17},{17,25},{2,10},{10,18},{18,26},{... | collective-permute-start | bytes 392 | tf_op jit(solution)/shard_map/while/body/eval_jaxpr/ppermute | solution.py:14
  193.2 21.4 %collective-permute-start = (bf16[32,512]{1,0:T(8,128)(2,1)S(1)}, bf16[32,512]{1,0:T(8,128)(2,1)S(1)}, u32[]{:S(2)}, u32[]{:S(2)}) collective-permute-start(bf16[32,512]{1,0:T(8,128)(2,1)S(1)} %get-tuple-element.395), channel_id=1, source_target_pairs={{0,8},{8,16},{16,24},{1,9},{9,17},{17,25},{2,10},{10,18},{18,26},{... | collective-permute-start | bytes 98312 | tf_op jit(solution)/shard_map/while/body/eval_jaxpr/ppermute | solution.py:14
  210.5 4.1 %collective-permute-start.1 = (f32[32]{0:T(128)S(1)}, f32[32]{0:T(128)S(1)}, u32[]{:S(2)}, u32[]{:S(2)}) collective-permute-start(f32[32]{0:T(128)S(1)} %get-tuple-element.399), channel_id=1, source_target_pairs={{0,8},{8,16},{16,24},{1,9},{9,17},{17,25},{2,10},{10,18},{18,26},{... | collective-permute-start | bytes 392 | tf_op jit(solution)/shard_map/while/body/eval_jaxpr/ppermute | solution.py:14
  239.7 21.4 %collective-permute-start = (bf16[32,512]{1,0:T(8,128)(2,1)S(1)}, bf16[32,512]{1,0:T(8,128)(2,1)S(1)}, u32[]{:S(2)}, u32[]{:S(2)}) collective-permute-start(bf16[32,512]{1,0:T(8,128)(2,1)S(1)} %get-tuple-element.395), channel_id=1, source_target_pairs={{0,8},{8,16},{16,24},{1,9},{9,17},{17,25},{2,10},{10,18},{18,26},{... | collective-permute-start | bytes 98312 | tf_op jit(solution)/shard_map/while/body/eval_jaxpr/ppermute | solution.py:14
  257.0 4.1 %collective-permute-start.1 = (f32[32]{0:T(128)S(1)}, f32[32]{0:T(128)S(1)}, u32[]{:S(2)}, u32[]{:S(2)}) collective-permute-start(f32[32]{0:T(128)S(1)} %get-tuple-element.399), channel_id=1, source_target_pairs={{0,8},{8,16},{16,24},{1,9},{9,17},{17,25},{2,10},{10,18},{18,26},{... | collective-permute-start | bytes 392 | tf_op jit(solution)/shard_map/while/body/eval_jaxpr/ppermute | solution.py:14
  286.3 21.4 %collective-permute-start = (bf16[32,512]{1,0:T(8,128)(2,1)S(1)}, bf16[32,512]{1,0:T(8,128)(2,1)S(1)}, u32[]{:S(2)}, u32[]{:S(2)}) collective-permute-start(bf16[32,512]{1,0:T(8,128)(2,1)S(1)} %get-tuple-element.395), channel_id=1, source_target_pairs={{0,8},{8,16},{16,24},{1,9},{9,17},{17,25},{2,10},{10,18},{18,26},{... | collective-permute-start | bytes 98312 | tf_op jit(solution)/shard_map/while/body/eval_jaxpr/ppermute | solution.py:14
  303.6 4.1 %collective-permute-start.1 = (f32[32]{0:T(128)S(1)}, f32[32]{0:T(128)S(1)}, u32[]{:S(2)}, u32[]{:S(2)}) collective-permute-start(f32[32]{0:T(128)S(1)} %get-tuple-element.399), channel_id=1, source_target_pairs={{0,8},{8,16},{16,24},{1,9},{9,17},{17,25},{2,10},{10,18},{18,26},{... | collective-permute-start | bytes 392 | tf_op jit(solution)/shard_map/while/body/eval_jaxpr/ppermute | solution.py:14
  332.9 21.4 %collective-permute-start = (bf16[32,512]{1,0:T(8,128)(2,1)S(1)}, bf16[32,512]{1,0:T(8,128)(2,1)S(1)}, u32[]{:S(2)}, u32[]{:S(2)}) collective-permute-start(bf16[32,512]{1,0:T(8,128)(2,1)S(1)} %get-tuple-element.395), channel_id=1, source_target_pairs={{0,8},{8,16},{16,24},{1,9},{9,17},{17,25},{2,10},{10,18},{18,26},{... | collective-permute-start | bytes 98312 | tf_op jit(solution)/shard_map/while/body/eval_jaxpr/ppermute | solution.py:14
  350.2 4.1 %collective-permute-start.1 = (f32[32]{0:T(128)S(1)}, f32[32]{0:T(128)S(1)}, u32[]{:S(2)}, u32[]{:S(2)}) collective-permute-start(f32[32]{0:T(128)S(1)} %get-tuple-element.399), channel_id=1, source_target_pairs={{0,8},{8,16},{16,24},{1,9},{9,17},{17,25},{2,10},{10,18},{18,26},{... | collective-permute-start | bytes 392 | tf_op jit(solution)/shard_map/while/body/eval_jaxpr/ppermute | solution.py:14
  354.3 0.5 copy-start
  354.3 0.5 copy-start.1
